TPU v7x, 32 devices: a whole 2x2x4 slice. The times are simulated.
32 devices in a mesh: row: 4 (over z), col: 8 (over y, x, core).
Axes of the slice: x: 2, y: 2, z: 4, core: 2. Of those that a mesh axis runs over, the one named last changes fastest.
Arguments:
- tokens_in: bfloat16 [8192, 1408], P(('row', 'col')), may hold values from -300 to 300
- ln1_gain: bfloat16 [1408], replicated, may hold values from 0.099609375 to 1.8984375
- ln1_bias: bfloat16 [1408], replicated, may hold values from -3 to 3
- qkv_weight: bfloat16 [1408, 4224], P('row', 'col'), may hold values from -0.8 to 0.8
- qkv_bias: bfloat16 [4224], P('col'), may hold values from -3 to 3
- proj_weight: bfloat16 [1408, 1408], P('col', 'row'), may hold values from -0.15625 to 0.15625
- proj_bias: bfloat16 [1408], replicated, may hold values from -3 to 3
- ln2_gain: bfloat16 [1408], replicated, may hold values from 0.099609375 to 1.8984375
- ln2_bias: bfloat16 [1408], replicated, may hold values from -3 to 3
- fc1_weight: bfloat16 [1408, 6144], P('row', 'col'), may hold values from -0.15625 to 0.15625
- fc1_bias: bfloat16 [6144], P('col'), may hold values from -3 to 3
- fc2_weight: bfloat16 [1408, 6144], P('row', 'col'), may hold values from -0.078125 to 0.078125
- fc2_bias: bfloat16 [1408], replicated, may hold values from -3 to 3
Outputs:
- tokens_out: bfloat16 [8192, 1408], P(('row', 'col'))
All inputs are finite; a program needn't handle non-finite values.
Results may differ from a plain program's by a relative error of at most 0.01.
Values may be sent and summed in bfloat16 or wider, within the bound.
A program may use at most 64 MiB of HBM per device.

v0:
```python
import jax
import jax.numpy as jnp
from jax import lax
from jax.sharding import PartitionSpec as P

HEADS = 16


def norm_local(values, gain, bias):
    mean = jnp.mean(values, axis=-1, keepdims=True)
    centred = values - mean
    var = jnp.mean(centred * centred, axis=-1, keepdims=True)
    return centred * lax.rsqrt(var + 1e-06) * gain.astype(jnp.float32) + bias.astype(jnp.float32)


def attend(qkv, heads):
    length = qkv.shape[0]
    head_size = qkv.shape[1] // (3 * heads)
    parts = qkv.reshape(length, heads, 3, head_size)
    query = parts[:, :, 0]
    keys = parts[:, :, 1]
    values = parts[:, :, 2]
    block = min(512, length)
    blocks = query.reshape(length // block, block, heads, head_size)
    scale = 1.0 / head_size**0.5

    def one_block(qblock):
        scores = (
            jnp.einsum("qhe,khe->hqk", qblock, keys, preferred_element_type=jnp.float32) * scale
        )
        top = jnp.max(scores, axis=-1, keepdims=True)
        expo = jnp.exp(scores - top)
        probs = (expo / jnp.sum(expo, axis=-1, keepdims=True)).astype(jnp.bfloat16)
        mixed = jnp.einsum("hqk,khe->qhe", probs, values, preferred_element_type=jnp.float32)
        return mixed.astype(jnp.bfloat16).reshape(block, heads * head_size)

    return lax.map(one_block, blocks).reshape(length, heads * head_size)


def project_back(left, right):
    return lax.dot_general(
        left, right, (((1,), (1,)), ((), ())), preferred_element_type=jnp.float32
    )


def local(
    tokens_in,
    ln1_gain,
    ln1_bias,
    qkv_weight,
    qkv_bias,
    proj_weight,
    proj_bias,
    ln2_gain,
    ln2_bias,
    fc1_weight,
    fc1_bias,
    fc2_weight,
    fc2_bias,
):
    local_heads = HEADS // lax.axis_size("col")
    own_rows = tokens_in.shape[0]
    inputs = tokens_in.astype(jnp.float32)
    qkv_full = lax.all_gather(qkv_weight, "row", axis=0, tiled=True)
    proj_full = lax.all_gather(proj_weight, "row", axis=1, tiled=True)
    fc1_full = lax.all_gather(fc1_weight, "row", axis=0, tiled=True)
    fc2_full = lax.all_gather(fc2_weight, "row", axis=0, tiled=True)
    qkv_shift = qkv_bias.astype(jnp.float32)
    fc1_shift = fc1_bias.astype(jnp.float32)
    ln1 = norm_local(inputs, ln1_gain, ln1_bias).astype(jnp.bfloat16)
    product = (
        jnp.dot(
            lax.all_gather(ln1, "col", axis=0, tiled=True),
            qkv_full,
            preferred_element_type=jnp.float32,
        )
        + qkv_shift
    )
    qkv = product.astype(jnp.bfloat16)
    attn = attend(qkv, local_heads)
    proj_whole = lax.all_gather(proj_full, "col", axis=0, tiled=True)
    groups = lax.axis_size("col")
    width = proj_whole.shape[0] // groups
    own_heads = lax.all_to_all(attn, "col", split_axis=0, concat_axis=1, tiled=True)
    lefts = own_heads.reshape(own_rows, groups, width)
    rights = proj_whole.reshape(groups, width, proj_whole.shape[1])
    group_parts = jnp.einsum("rgc,gcd->grd", lefts, rights, preferred_element_type=jnp.float32)
    group_parts = lax.optimization_barrier(group_parts.astype(jnp.bfloat16))
    attn_sum = jnp.sum(group_parts.astype(jnp.float32), axis=0)
    resid = inputs + attn_sum + proj_bias.astype(jnp.float32)
    ln2 = norm_local(resid, ln2_gain, ln2_bias).astype(jnp.bfloat16)
    product = (
        jnp.dot(
            lax.all_gather(ln2, "col", axis=0, tiled=True),
            fc1_full,
            preferred_element_type=jnp.float32,
        )
        + fc1_shift
    )
    hidden = jax.nn.gelu(product, approximate=False).astype(jnp.bfloat16)
    mlp_sum = lax.psum_scatter(
        project_back(hidden, fc2_full).astype(jnp.bfloat16), "col", scatter_dimension=0, tiled=True
    ).astype(jnp.float32)
    result = resid + mlp_sum + fc2_bias.astype(jnp.float32)
    return result.astype(jnp.bfloat16)


def solution(mesh):
    in_specs = (
        P(("row", "col"), None),
        P(),
        P(),
        P("row", "col"),
        P("col"),
        P("col", "row"),
        P(),
        P(),
        P(),
        P("row", "col"),
        P("col"),
        P("row", "col"),
        P(),
    )
    out_specs = P(("row", "col"), None)
    return jax.shard_map(local, mesh=mesh, in_specs=in_specs, out_specs=out_specs, check_vma=False)
```

profile of v0, /device:TPU:0, one launch (start us, length us, event | category | flops | bytes accessed | tf_op | source)
XLA Modules:
  0.0 374.7 jit_solution(7904936646565501967)
XLA Ops:
  8.7 1.3 convert_reduce_fusion.1
  10.0 1.4 fusion.37
  11.4 2.3 fusion.40
  13.8 25.0 %all-gather.1 = bf16[4,352,176]{1,2,0:T(8,128)(2,1)S(1)} all-gather(bf16[1,352,176]{1,2,0:T(8,128)(2,1)} %bitcast.70), channel_id=1, replica_groups=mesh['row'=4,'col'=8] {'row'}, dimensions={0}, use_global_device_ids=true | all-gather | bytes 619520 | tf_op jit(solution)/shard_map/all_gather | solution.py:65
  39.0 1.2 reshape.54
  41.4 14.3 %all-gather.19.cloned.1.call-done = bf16[4,352,528]{1,2,0:T(8,128)(2,1)} async-done(((bf16[1,352,528]{1,2,0:T(8,128)(2,1)}), bf16[4,352,528]{1,2,0:T(8,128)(2,1)}) %all-gather.19.cloned.1.call-update) | async-done | bytes 1486864 | tf_op jit(solution)/shard_map/all_gather | solution.py:64
  55.7 2.0 copy.24
  57.8 1.2 reshape.52
  58.9 41.5 %all-gather.9.cloned.1.call-done = bf16[2048,1408]{1,0:T(8,128)(2,1)} async-done(((bf16[256,1408]{1,0:T(8,128)(2,1)}), bf16[2048,1408]{1,0:T(8,128)(2,1)}) %all-gather.9.cloned.1.call-update) | async-done | bytes 5767184 | tf_op jit(solution)/shard_map/all_gather | solution.py:73
  100.5 6.4 %add_convert_fusion = bf16[2048,528]{0,1:T(8,128)(2,1)S(1)} fusion(bf16[2048,1408]{1,0:T(8,128)(2,1)} %all-gather.9.cloned.1.call-done, bf16[1408,528]{0,1:T(8,128)(2,1)S(1)} %reshape.52, f32[528]{0:T(1024)S(1)} %convert_element_type.67), kind=kOutput, calls=%fused_computation.40 | convolution fusion | flops 3047227392 | bytes 9418816 | tf_op jit(solution)/shard_map/dot_general | solution.py:72
  106.9 1.1 slice_bitcast_fusion
  108.7 48.0 %while.10 = (s32[]{:T(128)}, bf16[4,512,176]{1,2,0:T(8,128)(2,1)S(1)}, bf16[4,512,2,88]{1,3,2,0:T(8,128)(2,1)S(1)}, bf16[2048,2,88]{0,2,1:T(8,128)(2,1)}, bf16[2048,2,88]{0,2,1:T(8,128)(2,1)S(1)}, /*index=5*/s32[]{:T(128)}) while((s32[]{:T(128)}, bf16[4,512,176]{1,2,0:T(8,128)(2,1)S(1)}, bf16[4,512,2,88]{1,3,2,0:T(8,128)(2,1)S(1)}, ...), condition=%wide.region_5.6_spmd, body=%wide.region_2.5_spmd.sunk | while | flops 748775424 | bytes 18948172 | solution.py:37
  108.7 7.1 %fusion.96 = (f32[2,512]{1,0:T(2,128)S(1)}, f32[2,512,2048]{2,1,0:T(8,128)}) fusion(bf16[2048,2,88]{0,2,1:T(8,128)(2,1)} %get-tuple-element.108, bf16[4,512,2,88]{1,3,2,0:T(8,128)(2,1)S(1)} %get-tuple-element.107, s32[]{:T(128)} %get-tuple-element.99), kind=kOutput, calls=%fused_computation.93.clone.1 | convolution fusion | flops 375392256 | bytes 9293828 | tf_op jit(solution)/shard_map/while/body/eval_jaxpr/sub | solution.py:32
  115.9 4.9 %fusion.97 = bf16[2,512,88]{1,2,0:T(8,128)(2,1)S(1)} fusion(bf16[2048,2,88]{0,2,1:T(8,128)(2,1)S(1)} %get-tuple-element.109, f32[2,512,2048]{2,1,0:T(8,128)} %get-tuple-element.91, f32[2,512]{1,0:T(2,128)S(1)} %get-tuple-element.92), kind=kOutput, calls=%fused_computation.7.clone.1 | convolution fusion | flops 373383168 | bytes 9293824 | tf_op jit(solution)/shard_map/while/body/eval_jaxpr/hqk,khe->qhe/dot_general | solution.py:34
  120.8 7.0 %fusion.96 = (f32[2,512]{1,0:T(2,128)S(1)}, f32[2,512,2048]{2,1,0:T(8,128)}) fusion(bf16[2048,2,88]{0,2,1:T(8,128)(2,1)} %get-tuple-element.108, bf16[4,512,2,88]{1,3,2,0:T(8,128)(2,1)S(1)} %get-tuple-element.107, s32[]{:T(128)} %get-tuple-element.99), kind=kOutput, calls=%fused_computation.93.clone.1 | convolution fusion | flops 375392256 | bytes 9293828 | tf_op jit(solution)/shard_map/while/body/eval_jaxpr/sub | solution.py:32
  127.8 4.9 %fusion.97 = bf16[2,512,88]{1,2,0:T(8,128)(2,1)S(1)} fusion(bf16[2048,2,88]{0,2,1:T(8,128)(2,1)S(1)} %get-tuple-element.109, f32[2,512,2048]{2,1,0:T(8,128)} %get-tuple-element.91, f32[2,512]{1,0:T(2,128)S(1)} %get-tuple-element.92), kind=kOutput, calls=%fused_computation.7.clone.1 | convolution fusion | flops 373383168 | bytes 9293824 | tf_op jit(solution)/shard_map/while/body/eval_jaxpr/hqk,khe->qhe/dot_general | solution.py:34
  132.8 7.0 %fusion.96 = (f32[2,512]{1,0:T(2,128)S(1)}, f32[2,512,2048]{2,1,0:T(8,128)}) fusion(bf16[2048,2,88]{0,2,1:T(8,128)(2,1)} %get-tuple-element.108, bf16[4,512,2,88]{1,3,2,0:T(8,128)(2,1)S(1)} %get-tuple-element.107, s32[]{:T(128)} %get-tuple-element.99), kind=kOutput, calls=%fused_computation.93.clone.1 | convolution fusion | flops 375392256 | bytes 9293828 | tf_op jit(solution)/shard_map/while/body/eval_jaxpr/sub | solution.py:32
  139.8 4.9 %fusion.97 = bf16[2,512,88]{1,2,0:T(8,128)(2,1)S(1)} fusion(bf16[2048,2,88]{0,2,1:T(8,128)(2,1)S(1)} %get-tuple-element.109, f32[2,512,2048]{2,1,0:T(8,128)} %get-tuple-element.91, f32[2,512]{1,0:T(2,128)S(1)} %get-tuple-element.92), kind=kOutput, calls=%fused_computation.7.clone.1 | convolution fusion | flops 373383168 | bytes 9293824 | tf_op jit(solution)/shard_map/while/body/eval_jaxpr/hqk,khe->qhe/dot_general | solution.py:34
  144.7 7.1 %fusion.96 = (f32[2,512]{1,0:T(2,128)S(1)}, f32[2,512,2048]{2,1,0:T(8,128)}) fusion(bf16[2048,2,88]{0,2,1:T(8,128)(2,1)} %get-tuple-element.108, bf16[4,512,2,88]{1,3,2,0:T(8,128)(2,1)S(1)} %get-tuple-element.107, s32[]{:T(128)} %get-tuple-element.99), kind=kOutput, calls=%fused_computation.93.clone.1 | convolution fusion | flops 375392256 | bytes 9293828 | tf_op jit(solution)/shard_map/while/body/eval_jaxpr/sub | solution.py:32
  151.8 4.9 %fusion.97 = bf16[2,512,88]{1,2,0:T(8,128)(2,1)S(1)} fusion(bf16[2048,2,88]{0,2,1:T(8,128)(2,1)S(1)} %get-tuple-element.109, f32[2,512,2048]{2,1,0:T(8,128)} %get-tuple-element.91, f32[2,512]{1,0:T(2,128)S(1)} %get-tuple-element.92), kind=kOutput, calls=%fused_computation.7.clone.1 | convolution fusion | flops 373383168 | bytes 9293824 | tf_op jit(solution)/shard_map/while/body/eval_jaxpr/hqk,khe->qhe/dot_general | solution.py:34
  157.4 1.0 copy.30
  158.4 3.5 all-to-all-start
  162.3 11.4 %all-to-all-done = bf16[8,256,176]{1,2,0:T(8,128)(2,1)S(1)} async-done(((bf16[8,256,176]{1,2,0:T(8,128)(2,1)}), bf16[8,256,176]{1,2,0:T(8,128)(2,1)S(1)}, u32[]{:S(2)}, u32[]{:S(2)}) %all-to-all-start) | async-done | bytes 720928 | tf_op jit(solution)/shard_map/all_to_all | solution.py:84
  173.7 4.0 %convolution_convert_fusion.1 = bf16[8,256,1408]{2,1,0:T(8,128)(2,1)S(1)} fusion(bf16[8,176,1408]{2,1,0:T(8,128)(2,1)} %bitcast.66, bf16[8,256,176]{1,2,0:T(8,128)(2,1)S(1)} %all-to-all-done), kind=kOutput, calls=%fused_computation.39 | convolution fusion | flops 1017905152 | bytes 10452992 | tf_op jit(solution)/shard_map/rgc,gcd->grd/dot_general | solution.py:87
  177.8 0.8 convert_reduce_fusion
  179.3 1.3 add_convert_fusion.2
  180.7 5.5 %all-gather.15.cloned.1.call-done = bf16[1408,768]{1,0:T(8,128)(2,1)} async-done(((bf16[352,768]{1,0:T(8,128)(2,1)}), bf16[1408,768]{1,0:T(8,128)(2,1)}) %all-gather.15.cloned.1.call-update) | async-done | bytes 2162704 | tf_op jit(solution)/shard_map/all_gather | solution.py:66
  186.2 47.0 %all-gather.17.cloned.1.call-done = bf16[1408,768]{1,0:T(8,128)(2,1)} async-done(((bf16[352,768]{1,0:T(8,128)(2,1)}), bf16[1408,768]{1,0:T(8,128)(2,1)}) %all-gather.17.cloned.1.call-update) | async-done | bytes 2162704 | tf_op jit(solution)/shard_map/all_gather | solution.py:67
  233.2 43.7 %all-gather.13.cloned.1.call-done = bf16[2048,1408]{1,0:T(8,128)(2,1)} async-done(((bf16[256,1408]{1,0:T(8,128)(2,1)}), bf16[2048,1408]{1,0:T(8,128)(2,1)}) %all-gather.13.cloned.1.call-update) | async-done | bytes 5767184 | tf_op jit(solution)/shard_map/all_gather | solution.py:94
  276.9 29.4 %convolution_convert_fusion = bf16[2048,1408]{1,0:T(8,128)(2,1)} fusion(bf16[1408,768]{1,0:T(8,128)(2,1)} %all-gather.17.cloned.1.call-done, bf16[2048,1408]{1,0:T(8,128)(2,1)} %all-gather.13.cloned.1.call-done, bf16[1408,768]{1,0:T(8,128)(2,1)} %all-gather.15.cloned.1.call-done, f32[768]{0:T(1024)S(1)} %convert_element_type.75), kind=kOutput, calls=%fused_computation.20 | convolution fusion | flops 8965062656 | bytes 15862784 | tf_op jit(solution)/shard_map/dot_general | solution.py:41
  306.4 59.1 %reduce-scatter.2.cloned.1.call-done = bf16[256,1408]{1,0:T(8,128)(2,1)} async-done(((bf16[2048,1408]{1,0:T(8,128)(2,1)}), bf16[256,1408]{1,0:T(8,128)(2,1)}) %reduce-scatter.2.cloned.1.call-update) | async-done | bytes 720912 | tf_op jit(solution)/shard_map/reduce_scatter | solution.py:101
  365.5 2.3 add_convert_fusion.1
  (55 shorter events, 6.1 us)
Async XLA Ops:
  6.5 34.8 %copy-start.6 = (bf16[528]{0:T(1024)(128)(2,1)S(1)}, bf16[528]{0:T(1024)(128)(2,1)}, u32[]{:S(2)}) copy-start(bf16[528]{0:T(1024)(128)(2,1)} %param.19) | copy-start | bytes 3172
  6.5 49.2 %all-gather.19.cloned.1.call-start = ((), (), s32[]{:S(2)}) async-start(), calls=%async_computation.8 | async-start | bytes 2027520 | tf_op jit(solution)/shard_map/all_gather | solution.py:64
  7.3 93.2 %all-gather.9.cloned.1.call-start = ((), (), s32[]{:S(2)}) async-start(), calls=%async_computation.2 | async-start | bytes 6488064 | tf_op jit(solution)/shard_map/all_gather | solution.py:73
  13.8 148.5 %all-gather.11.cloned.1.call-start = ((), (), s32[]{:S(2)}) async-start(), calls=%async_computation.3 | async-start | bytes 4460544 | tf_op jit(solution)/shard_map/all_gather | solution.py:81
  40.2 146.0 %all-gather.15.cloned.1.call-start = ((), (), s32[]{:S(2)}) async-start(), calls=%async_computation.5 | async-start | bytes 2703360 | tf_op jit(solution)/shard_map/all_gather | solution.py:66
  40.8 192.4 %all-gather.17.cloned.1.call-start = ((), (), s32[]{:S(2)}) async-start(), calls=%async_computation.6 | async-start | bytes 2703360 | tf_op jit(solution)/shard_map/all_gather | solution.py:67
  106.9 1.8 copy-start.1
  108.7 53.5 %copy-start.2 = (bf16[1408]{0:T(1024)(128)(2,1)S(1)}, bf16[1408]{0:T(1024)(128)(2,1)}, u32[]{:S(2)}) copy-start(bf16[1408]{0:T(1024)(128)(2,1)} %param.21) | copy-start | bytes 8452
  108.7 53.5 %copy-start.3 = (bf16[1408]{0:T(1024)(128)(2,1)S(1)}, bf16[1408]{0:T(1024)(128)(2,1)}, u32[]{:S(2)}) copy-start(bf16[1408]{0:T(1024)(128)(2,1)} %param.22) | copy-start | bytes 8452
  108.7 53.5 %copy-start.4 = (bf16[1408]{0:T(1024)(128)(2,1)S(1)}, bf16[1408]{0:T(1024)(128)(2,1)}, u32[]{:S(2)}) copy-start(bf16[1408]{0:T(1024)(128)(2,1)} %param.23) | copy-start | bytes 8452
  158.4 15.3 %all-to-all-start = ((bf16[8,256,176]{1,2,0:T(8,128)(2,1)}), bf16[8,256,176]{1,2,0:T(8,128)(2,1)S(1)}, u32[]{:S(2)}, u32[]{:S(2)}) async-start(bf16[8,256,176]{1,2,0:T(8,128)(2,1)} %copy.30), calls=%async_computation | async-start | bytes 1441792 | tf_op jit(solution)/shard_map/all_to_all | solution.py:84
  162.0 114.9 %all-gather.13.cloned.1.call-start = ((), (), s32[]{:S(2)}) async-start(), calls=%async_computation.4 | async-start | bytes 6488064 | tf_op jit(solution)/shard_map/all_gather | solution.py:94
  173.7 4.9 %copy-start = (bf16[256,1408]{1,0:T(8,128)(2,1)S(1)}, bf16[256,1408]{1,0:T(8,128)(2,1)}, u32[]{:S(2)}) copy-start(bf16[256,1408]{1,0:T(8,128)(2,1)} %param.15) | copy-start | bytes 2162692
  177.8 2.9 copy-start.7
  180.6 184.9 %reduce-scatter.2.cloned.1.call-start = ((), (), s32[]{:S(2)}) async-start(), calls=%async_computation.7 | async-start | bytes 6488064 | tf_op jit(solution)/shard_map/reduce_scatter | solution.py:101
  180.7 125.7 %copy-start.5 = (bf16[1408]{0:T(1024)(128)(2,1)S(1)}, bf16[1408]{0:T(1024)(128)(2,1)}, u32[]{:S(2)}) copy-start(bf16[1408]{0:T(1024)(128)(2,1)} %param.27) | copy-start | bytes 8452
Sparse Core Ops, SparseCore 0:
  8.9 46.7 all-gather.18
  57.6 42.8 all-gather.8
  102.4 35.6 all-gather.10
  139.4 46.7 all-gather.14
  187.6 45.5 all-gather.16
  234.9 41.9 all-gather.12
  306.5 58.9 reduce-scatter.1
where the time goes:
time: 375 us
  waiting for transfers between devices  225 us (60%)
  matrix products  87.7 us (23%)
  blocking collectives  25 us (7%)
  between operations  13.8 us (4%)
  other arithmetic  11.5 us (3%)
  local copies, waits for them, and re-layouts  8.19 us (2%)
  starting transfers between devices  3.97 us (1%)
    reduce_scatter x1, waiting for transfers between devices, local(): lax.psum_scatter(project_back(hidden, fc2_full).astype(jnp.bfloat16), 'co...  59.1 us
    all_gather x1, waiting for transfers between devices, local(): fc2_full = lax.all_gather(fc2_weight, 'row', axis=0, tiled=True)  47 us
    all_gather x1, waiting for transfers between devices, local(): lax.all_gather(ln2, 'col', axis=0, tiled=True)  43.7 us
    all_gather x1, waiting for transfers between devices, local(): lax.all_gather(ln1, 'col', axis=0, tiled=True)  41.5 us
    dot_general x1, matrix products, project_back(): lax.dot_general(left, right, (((1,), (1,)), ((), ())), preferred_element_...  29.4 us
    sub x4, matrix products, one_block(): expo = jnp.exp(scores - top)  28.3 us
    all_gather x1, blocking collectives, local(): proj_full = lax.all_gather(proj_weight, 'row', axis=1, tiled=True)  25 us
    dot_general x4, matrix products, one_block(): jnp.einsum('hqk,khe->qhe', probs, values, preferred_element_type=jnp.floa...  19.5 us
  transfers between devices with their start and end apart: 8, of which 7 were waited for; matrix products, arithmetic and copies ran while one was open for 20% of the time, Pallas kernels for 0%

commit v1 on v0

--- a/solution.py
+++ b/solution.py
@@ -62,7 +62,7 @@
     own_rows = tokens_in.shape[0]
     inputs = tokens_in.astype(jnp.float32)
     qkv_full = lax.all_gather(qkv_weight, "row", axis=0, tiled=True)
-    proj_full = lax.all_gather(proj_weight, "row", axis=1, tiled=True)
+    proj_full = jnp.concatenate(lax.all_gather(proj_weight, axis_name="row"), axis=1)
     fc1_full = lax.all_gather(fc1_weight, "row", axis=0, tiled=True)
     fc2_full = lax.all_gather(fc2_weight, "row", axis=0, tiled=True)
     qkv_shift = qkv_bias.astype(jnp.float32)

time: 375 us -> 375 us (level)
  no operation moved by 1% of the time
where the time goes in v1:
time: 375 us
  waiting for transfers between devices  225 us (60%)
  matrix products  87.7 us (23%)
  blocking collectives  25 us (7%)
  between operations  13.8 us (4%)
  other arithmetic  11.5 us (3%)
  local copies, waits for them, and re-layouts  8.19 us (2%)
  starting transfers between devices  3.97 us (1%)
    reduce_scatter x1, waiting for transfers between devices, local(): lax.psum_scatter(project_back(hidden, fc2_full).astype(jnp.bfloat16), 'co...  59.1 us
    all_gather x1, waiting for transfers between devices, local(): fc2_full = lax.all_gather(fc2_weight, 'row', axis=0, tiled=True)  47 us
    all_gather x1, waiting for transfers between devices, local(): lax.all_gather(ln2, 'col', axis=0, tiled=True)  43.7 us
    all_gather x1, waiting for transfers between devices, local(): lax.all_gather(ln1, 'col', axis=0, tiled=True)  41.5 us
    dot_general x1, matrix products, project_back(): lax.dot_general(left, right, (((1,), (1,)), ((), ())), preferred_element_...  29.4 us
    sub x4, matrix products, one_block(): expo = jnp.exp(scores - top)  28.3 us
    all_gather x1, blocking collectives, local(): lax.all_gather(proj_weight, axis_name='row')  25 us
    dot_general x4, matrix products, one_block(): jnp.einsum('hqk,khe->qhe', probs, values, preferred_element_type=jnp.floa...  19.5 us
  transfers between devices with their start and end apart: 8, of which 7 were waited for; matrix products, arithmetic and copies ran while one was open for 20% of the time, Pallas kernels for 0%

profile of v1, /device:TPU:0, one launch (start us, length us, event | category | flops | bytes accessed | tf_op | source)
XLA Modules:
  0.0 374.7 jit_solution(9084854517247199095)
XLA Ops:
  8.7 1.3 convert_reduce_fusion.1
  10.0 1.4 fusion.37
  11.4 2.3 fusion.40
  13.8 25.0 %all-gather = bf16[704,352]{1,0:T(8,128)(2,1)S(1)} all-gather(bf16[176,352]{1,0:T(8,128)(2,1)} %param.20), channel_id=2, replica_groups=mesh['row'=4,'col'=8] {'row'}, dimensions={0}, use_global_device_ids=true | all-gather | bytes 619520 | tf_op jit(solution)/shard_map/all_gather | solution.py:65
  39.0 1.2 reshape.57
  41.4 14.3 %all-gather.19.cloned.1.call-done = bf16[4,352,528]{1,2,0:T(8,128)(2,1)} async-done(((bf16[1,352,528]{1,2,0:T(8,128)(2,1)}), bf16[4,352,528]{1,2,0:T(8,128)(2,1)}) %all-gather.19.cloned.1.call-update) | async-done | bytes 1486864 | tf_op jit(solution)/shard_map/all_gather | solution.py:64
  55.7 2.0 copy.25
  57.8 1.2 reshape.61
  58.9 41.5 %all-gather.9.cloned.1.call-done = bf16[2048,1408]{1,0:T(8,128)(2,1)} async-done(((bf16[256,1408]{1,0:T(8,128)(2,1)}), bf16[2048,1408]{1,0:T(8,128)(2,1)}) %all-gather.9.cloned.1.call-update) | async-done | bytes 5767184 | tf_op jit(solution)/shard_map/all_gather | solution.py:73
  100.5 6.4 %add_convert_fusion = bf16[2048,528]{0,1:T(8,128)(2,1)S(1)} fusion(bf16[2048,1408]{1,0:T(8,128)(2,1)} %all-gather.9.cloned.1.call-done, bf16[1408,528]{0,1:T(8,128)(2,1)S(1)} %reshape.61, f32[528]{0:T(1024)S(1)} %convert_element_type.67), kind=kOutput, calls=%fused_computation.40 | convolution fusion | flops 3047227392 | bytes 9418816 | tf_op jit(solution)/shard_map/dot_general | solution.py:72
  106.9 1.1 slice_bitcast_fusion
  108.7 48.0 %while.10 = (s32[]{:T(128)}, bf16[4,512,176]{1,2,0:T(8,128)(2,1)S(1)}, bf16[4,512,2,88]{1,3,2,0:T(8,128)(2,1)S(1)}, bf16[2048,2,88]{0,2,1:T(8,128)(2,1)}, bf16[2048,2,88]{0,2,1:T(8,128)(2,1)S(1)}, /*index=5*/s32[]{:T(128)}) while((s32[]{:T(128)}, bf16[4,512,176]{1,2,0:T(8,128)(2,1)S(1)}, bf16[4,512,2,88]{1,3,2,0:T(8,128)(2,1)S(1)}, ...), condition=%wide.region_5.6_spmd, body=%wide.region_2.5_spmd.sunk | while | flops 748775424 | bytes 18948172 | solution.py:37
  108.7 7.1 %fusion.96 = (f32[2,512]{1,0:T(2,128)S(1)}, f32[2,512,2048]{2,1,0:T(8,128)}) fusion(bf16[2048,2,88]{0,2,1:T(8,128)(2,1)} %get-tuple-element.108, bf16[4,512,2,88]{1,3,2,0:T(8,128)(2,1)S(1)} %get-tuple-element.107, s32[]{:T(128)} %get-tuple-element.99), kind=kOutput, calls=%fused_computation.93.clone.1 | convolution fusion | flops 375392256 | bytes 9293828 | tf_op jit(solution)/shard_map/while/body/eval_jaxpr/sub | solution.py:32
  115.9 4.9 %fusion.97 = bf16[2,512,88]{1,2,0:T(8,128)(2,1)S(1)} fusion(bf16[2048,2,88]{0,2,1:T(8,128)(2,1)S(1)} %get-tuple-element.109, f32[2,512,2048]{2,1,0:T(8,128)} %get-tuple-element.91, f32[2,512]{1,0:T(2,128)S(1)} %get-tuple-element.92), kind=kOutput, calls=%fused_computation.7.clone.1 | convolution fusion | flops 373383168 | bytes 9293824 | tf_op jit(solution)/shard_map/while/body/eval_jaxpr/hqk,khe->qhe/dot_general | solution.py:34
  120.8 7.0 %fusion.96 = (f32[2,512]{1,0:T(2,128)S(1)}, f32[2,512,2048]{2,1,0:T(8,128)}) fusion(bf16[2048,2,88]{0,2,1:T(8,128)(2,1)} %get-tuple-element.108, bf16[4,512,2,88]{1,3,2,0:T(8,128)(2,1)S(1)} %get-tuple-element.107, s32[]{:T(128)} %get-tuple-element.99), kind=kOutput, calls=%fused_computation.93.clone.1 | convolution fusion | flops 375392256 | bytes 9293828 | tf_op jit(solution)/shard_map/while/body/eval_jaxpr/sub | solution.py:32
  127.8 4.9 %fusion.97 = bf16[2,512,88]{1,2,0:T(8,128)(2,1)S(1)} fusion(bf16[2048,2,88]{0,2,1:T(8,128)(2,1)S(1)} %get-tuple-element.109, f32[2,512,2048]{2,1,0:T(8,128)} %get-tuple-element.91, f32[2,512]{1,0:T(2,128)S(1)} %get-tuple-element.92), kind=kOutput, calls=%fused_computation.7.clone.1 | convolution fusion | flops 373383168 | bytes 9293824 | tf_op jit(solution)/shard_map/while/body/eval_jaxpr/hqk,khe->qhe/dot_general | solution.py:34
  132.8 7.0 %fusion.96 = (f32[2,512]{1,0:T(2,128)S(1)}, f32[2,512,2048]{2,1,0:T(8,128)}) fusion(bf16[2048,2,88]{0,2,1:T(8,128)(2,1)} %get-tuple-element.108, bf16[4,512,2,88]{1,3,2,0:T(8,128)(2,1)S(1)} %get-tuple-element.107, s32[]{:T(128)} %get-tuple-element.99), kind=kOutput, calls=%fused_computation.93.clone.1 | convolution fusion | flops 375392256 | bytes 9293828 | tf_op jit(solution)/shard_map/while/body/eval_jaxpr/sub | solution.py:32
  139.8 4.9 %fusion.97 = bf16[2,512,88]{1,2,0:T(8,128)(2,1)S(1)} fusion(bf16[2048,2,88]{0,2,1:T(8,128)(2,1)S(1)} %get-tuple-element.109, f32[2,512,2048]{2,1,0:T(8,128)} %get-tuple-element.91, f32[2,512]{1,0:T(2,128)S(1)} %get-tuple-element.92), kind=kOutput, calls=%fused_computation.7.clone.1 | convolution fusion | flops 373383168 | bytes 9293824 | tf_op jit(solution)/shard_map/while/body/eval_jaxpr/hqk,khe->qhe/dot_general | solution.py:34
  144.7 7.1 %fusion.96 = (f32[2,512]{1,0:T(2,128)S(1)}, f32[2,512,2048]{2,1,0:T(8,128)}) fusion(bf16[2048,2,88]{0,2,1:T(8,128)(2,1)} %get-tuple-element.108, bf16[4,512,2,88]{1,3,2,0:T(8,128)(2,1)S(1)} %get-tuple-element.107, s32[]{:T(128)} %get-tuple-element.99), kind=kOutput, calls=%fused_computation.93.clone.1 | convolution fusion | flops 375392256 | bytes 9293828 | tf_op jit(solution)/shard_map/while/body/eval_jaxpr/sub | solution.py:32
  151.8 4.9 %fusion.97 = bf16[2,512,88]{1,2,0:T(8,128)(2,1)S(1)} fusion(bf16[2048,2,88]{0,2,1:T(8,128)(2,1)S(1)} %get-tuple-element.109, f32[2,512,2048]{2,1,0:T(8,128)} %get-tuple-element.91, f32[2,512]{1,0:T(2,128)S(1)} %get-tuple-element.92), kind=kOutput, calls=%fused_computation.7.clone.1 | convolution fusion | flops 373383168 | bytes 9293824 | tf_op jit(solution)/shard_map/while/body/eval_jaxpr/hqk,khe->qhe/dot_general | solution.py:34
  157.4 1.0 copy.31
  158.4 3.5 all-to-all-start
  162.3 11.4 %all-to-all-done = bf16[8,256,176]{1,2,0:T(8,128)(2,1)S(1)} async-done(((bf16[8,256,176]{1,2,0:T(8,128)(2,1)}), bf16[8,256,176]{1,2,0:T(8,128)(2,1)S(1)}, u32[]{:S(2)}, u32[]{:S(2)}) %all-to-all-start) | async-done | bytes 720928 | tf_op jit(solution)/shard_map/all_to_all | solution.py:84
  173.7 4.0 %convolution_convert_fusion.1 = bf16[8,256,1408]{2,1,0:T(8,128)(2,1)S(1)} fusion(bf16[8,176,1408]{2,1,0:T(8,128)(2,1)} %bitcast.63, bf16[8,256,176]{1,2,0:T(8,128)(2,1)S(1)} %all-to-all-done), kind=kOutput, calls=%fused_computation.39 | convolution fusion | flops 1017905152 | bytes 10452992 | tf_op jit(solution)/shard_map/rgc,gcd->grd/dot_general | solution.py:87
  177.8 0.8 convert_reduce_fusion
  179.3 1.3 add_convert_fusion.2
  180.7 5.5 %all-gather.15.cloned.1.call-done = bf16[1408,768]{1,0:T(8,128)(2,1)} async-done(((bf16[352,768]{1,0:T(8,128)(2,1)}), bf16[1408,768]{1,0:T(8,128)(2,1)}) %all-gather.15.cloned.1.call-update) | async-done | bytes 2162704 | tf_op jit(solution)/shard_map/all_gather | solution.py:66
  186.2 47.0 %all-gather.17.cloned.1.call-done = bf16[1408,768]{1,0:T(8,128)(2,1)} async-done(((bf16[352,768]{1,0:T(8,128)(2,1)}), bf16[1408,768]{1,0:T(8,128)(2,1)}) %all-gather.17.cloned.1.call-update) | async-done | bytes 2162704 | tf_op jit(solution)/shard_map/all_gather | solution.py:67
  233.2 43.7 %all-gather.13.cloned.1.call-done = bf16[2048,1408]{1,0:T(8,128)(2,1)} async-done(((bf16[256,1408]{1,0:T(8,128)(2,1)}), bf16[2048,1408]{1,0:T(8,128)(2,1)}) %all-gather.13.cloned.1.call-update) | async-done | bytes 5767184 | tf_op jit(solution)/shard_map/all_gather | solution.py:94
  276.9 29.4 %convolution_convert_fusion = bf16[2048,1408]{1,0:T(8,128)(2,1)} fusion(bf16[1408,768]{1,0:T(8,128)(2,1)} %all-gather.17.cloned.1.call-done, bf16[2048,1408]{1,0:T(8,128)(2,1)} %all-gather.13.cloned.1.call-done, bf16[1408,768]{1,0:T(8,128)(2,1)} %all-gather.15.cloned.1.call-done, f32[768]{0:T(1024)S(1)} %convert_element_type.75), kind=kOutput, calls=%fused_computation.20 | convolution fusion | flops 8965062656 | bytes 15862784 | tf_op jit(solution)/shard_map/dot_general | solution.py:41
  306.4 59.1 %reduce-scatter.2.cloned.1.call-done = bf16[256,1408]{1,0:T(8,128)(2,1)} async-done(((bf16[2048,1408]{1,0:T(8,128)(2,1)}), bf16[256,1408]{1,0:T(8,128)(2,1)}) %reduce-scatter.2.cloned.1.call-update) | async-done | bytes 720912 | tf_op jit(solution)/shard_map/reduce_scatter | solution.py:101
  365.5 2.3 add_convert_fusion.1
  (55 shorter events, 6.1 us)
Async XLA Ops:
  6.5 34.8 %copy-start.6 = (bf16[528]{0:T(1024)(128)(2,1)S(1)}, bf16[528]{0:T(1024)(128)(2,1)}, u32[]{:S(2)}) copy-start(bf16[528]{0:T(1024)(128)(2,1)} %param.19) | copy-start | bytes 3172
  6.5 49.2 %all-gather.19.cloned.1.call-start = ((), (), s32[]{:S(2)}) async-start(), calls=%async_computation.8 | async-start | bytes 2027520 | tf_op jit(solution)/shard_map/all_gather | solution.py:64
  7.3 93.2 %all-gather.9.cloned.1.call-start = ((), (), s32[]{:S(2)}) async-start(), calls=%async_computation.2 | async-start | bytes 6488064 | tf_op jit(solution)/shard_map/all_gather | solution.py:73
  13.8 148.5 %all-gather.11.cloned.1.call-start = ((), (), s32[]{:S(2)}) async-start(), calls=%async_computation.3 | async-start | bytes 4460544 | tf_op jit(solution)/shard_map/all_gather | solution.py:81
  40.2 146.0 %all-gather.15.cloned.1.call-start = ((), (), s32[]{:S(2)}) async-start(), calls=%async_computation.5 | async-start | bytes 2703360 | tf_op jit(solution)/shard_map/all_gather | solution.py:66
  40.8 192.4 %all-gather.17.cloned.1.call-start = ((), (), s32[]{:S(2)}) async-start(), calls=%async_computation.6 | async-start | bytes 2703360 | tf_op jit(solution)/shard_map/all_gather | solution.py:67
  106.9 1.8 copy-start.1
  108.7 53.5 %copy-start.2 = (bf16[1408]{0:T(1024)(128)(2,1)S(1)}, bf16[1408]{0:T(1024)(128)(2,1)}, u32[]{:S(2)}) copy-start(bf16[1408]{0:T(1024)(128)(2,1)} %param.21) | copy-start | bytes 8452
  108.7 53.5 %copy-start.3 = (bf16[1408]{0:T(1024)(128)(2,1)S(1)}, bf16[1408]{0:T(1024)(128)(2,1)}, u32[]{:S(2)}) copy-start(bf16[1408]{0:T(1024)(128)(2,1)} %param.22) | copy-start | bytes 8452
  108.7 53.5 %copy-start.4 = (bf16[1408]{0:T(1024)(128)(2,1)S(1)}, bf16[1408]{0:T(1024)(128)(2,1)}, u32[]{:S(2)}) copy-start(bf16[1408]{0:T(1024)(128)(2,1)} %param.23) | copy-start | bytes 8452
  158.4 15.3 %all-to-all-start = ((bf16[8,256,176]{1,2,0:T(8,128)(2,1)}), bf16[8,256,176]{1,2,0:T(8,128)(2,1)S(1)}, u32[]{:S(2)}, u32[]{:S(2)}) async-start(bf16[8,256,176]{1,2,0:T(8,128)(2,1)} %copy.31), calls=%async_computation | async-start | bytes 1441792 | tf_op jit(solution)/shard_map/all_to_all | solution.py:84
  162.0 114.9 %all-gather.13.cloned.1.call-start = ((), (), s32[]{:S(2)}) async-start(), calls=%async_computation.4 | async-start | bytes 6488064 | tf_op jit(solution)/shard_map/all_gather | solution.py:94
  173.7 4.9 %copy-start = (bf16[256,1408]{1,0:T(8,128)(2,1)S(1)}, bf16[256,1408]{1,0:T(8,128)(2,1)}, u32[]{:S(2)}) copy-start(bf16[256,1408]{1,0:T(8,128)(2,1)} %param.15) | copy-start | bytes 2162692
  177.8 2.9 copy-start.7
  180.6 184.9 %reduce-scatter.2.cloned.1.call-start = ((), (), s32[]{:S(2)}) async-start(), calls=%async_computation.7 | async-start | bytes 6488064 | tf_op jit(solution)/shard_map/reduce_scatter | solution.py:101
  180.7 125.7 %copy-start.5 = (bf16[1408]{0:T(1024)(128)(2,1)S(1)}, bf16[1408]{0:T(1024)(128)(2,1)}, u32[]{:S(2)}) copy-start(bf16[1408]{0:T(1024)(128)(2,1)} %param.27) | copy-start | bytes 8452
Sparse Core Ops, SparseCore 0:
  8.9 46.7 all-gather.18
  57.6 42.8 all-gather.8
  102.4 35.6 all-gather.10
  139.4 46.7 all-gather.14
  187.6 45.5 all-gather.16
  234.9 41.9 all-gather.12
  306.5 58.9 reduce-scatter.1
